TPU v7x, 512 devices: a whole 4x4x16 slice. The times are simulated.
512 devices in a mesh: dp: 4 (over y), tensor: 8 (over z_hi, x), enc: 16 (over z_lo, core).
Axes of the slice: x: 4, y: 4, z: 16 (z_hi: 2, z_lo: 8; z = z_hi * 8 + z_lo), core: 2. Of those that a mesh axis runs over, the one named last changes fastest.
Arguments:
- span_states: bfloat16 [8192, 8192], P(('dp', 'enc'), 'tensor'), may hold values from -6 to 6
- neighbours: bfloat16 [128, 256, 1024], P(('dp', 'enc'), None, 'tensor'), may hold values from -6 to 6
- lengths: int32 [4], P('dp'), may hold values from 1 to 2048, 4096 in all
- wq_enc: bfloat16 [1024, 1024], P('enc', 'tensor')
- wk_enc: bfloat16 [8192, 1024], P('enc', 'tensor'), may hold values from -0.0625 to 0.0625
- wv_enc: bfloat16 [8192, 1024], P('enc', 'tensor'), may hold values from -0.0625 to 0.0625
- wo_enc: bfloat16 [1024, 1024], P('enc', 'tensor'), may hold values from -0.1875 to 0.1875
- wk_dec: bfloat16 [1024, 8192], P(('dp', 'enc'), 'tensor'), may hold values from -0.1875 to 0.1875
- wv_dec: bfloat16 [1024, 8192], P(('dp', 'enc'), 'tensor'), may hold values from -0.1875 to 0.1875
- queries: bfloat16 [8192, 8192], P(('dp', 'enc'), 'tensor'), may hold values from -6 to 6
- grad_out: bfloat16 [8192, 8192], P(('dp', 'enc'), 'tensor'), may hold values from -6 to 6
Outputs:
- attended: bfloat16 [8192, 8192], P(('dp', 'enc'), 'tensor')
- grad_encoded: float32 [128, 256, 1024], P(('dp', 'enc'), None, 'tensor')
Inputs may be any that keep to these rules, and one draw needn't show every extreme that they name: `lengths`: some sequence is live over all 2048 tokens.
All inputs are finite; a program needn't handle non-finite values. No bound on the sum of `lengths` on one device may be relied on, other than what follows from the above.
Results may differ from a plain program's by a relative error of at most 0.019.
Values may be sent and summed in bfloat16 or wider, within the bound.
A program may use at most 64 MiB of HBM per device.

v0:
```python
import math
import jax
import jax.numpy as jnp
from jax import lax
from jax.sharding import Mesh
from jax.sharding import PartitionSpec as P

HD = 128
EH = 64
TENSOR = ("tensor_0", "tensor_1")


def in_order(blocks, dim):
    dims = list(blocks.shape[1:])
    dims[dim] *= blocks.shape[0]
    return jnp.moveaxis(blocks, 0, dim).reshape(dims)


def one_gather(arrays, axis, dims):
    vector = jnp.concatenate([a.reshape(-1) for a in arrays])
    lines, at, gathered = (lax.all_gather(vector, axis), 0, [])
    for a, dim in zip(arrays, dims):
        blocks = lines[:, at : at + a.size].reshape(-1, *a.shape)
        gathered.append(in_order(blocks, dim))
        at += a.size
    return tuple(gathered)


def copy_for_each(x, axis):
    copies = jnp.broadcast_to(x, (lax.axis_size(axis), *x.shape))
    return lax.all_to_all(copies, axis, split_axis=0, concat_axis=0, tiled=True)


def gathered_copies(x, axis, dim):
    blocks = copy_for_each(x, axis)
    return in_order(blocks, dim)


def in_one_piece(arrays, axis, dim, along):
    both = jnp.concatenate(arrays, axis=along)
    filled, at, gathered = (lax.all_gather(both, axis, axis=dim, tiled=True), 0, [])
    for a in arrays:
        gathered.append(lax.slice_in_dim(filled, at, at + a.shape[along], axis=along))
        at += a.shape[along]
    return tuple(gathered)


def from_behind(value, axis, steps):
    count = lax.axis_size(axis)
    first, last = (max(0, -steps), min(count, count - steps))
    return lax.ppermute(value, axis, [(source, source + steps) for source in range(first, last)])


def sum_in_order(blocks, axes, turns):
    inside = blocks.shape[1:]
    blocks = blocks.reshape(*(lax.axis_size(a) for a in axes), *inside)
    blocks = jnp.moveaxis(blocks, turns, range(len(axes))).reshape(-1, *inside)
    for k in turns:
        blocks = lax.psum_scatter(blocks, axes[k], scatter_dimension=0, tiled=True)
    return blocks[0]


def in_blocks(x, dim, count):
    before, after = (x.shape[:dim], x.shape[dim + 1 :])
    return jnp.moveaxis(x.reshape(*before, count, -1, *after), dim, 0)


def summed_rows(x, axes, turns, dim):
    count = lax.axis_size(axes)
    return sum_in_order(in_blocks(x, dim, count), axes, turns)


def on_device(
    span_states,
    neighbours,
    lengths,
    wq_enc,
    wk_enc,
    wv_enc,
    wo_enc,
    wk_dec,
    wv_dec,
    queries,
    grad_out,
):
    spans, keys_each, width = neighbours.shape
    row_count = span_states.shape[0]
    span_len = row_count // spans
    key_rows = spans * keys_each
    flat_neighbour = neighbours.reshape(key_rows, width)
    full_states, full_neighbour = one_gather((span_states, flat_neighbour), TENSOR, (1, 1))
    sliced = full_neighbour
    query_sum = jnp.dot(
        sliced, gathered_copies(wq_enc, "enc", 0), preferred_element_type=jnp.float32
    )
    segments = in_one_piece((wk_enc, wv_enc), "enc", 0, 1)
    sliced = full_states
    key_sum = jnp.dot(sliced, segments[0], preferred_element_type=jnp.float32)
    value_sum = jnp.dot(sliced, segments[1], preferred_element_type=jnp.float32)
    heads_enc = width // EH
    query_heads = query_sum.astype(jnp.bfloat16).reshape(spans, keys_each, heads_enc, EH)
    key_heads = key_sum.astype(jnp.bfloat16).reshape(spans, span_len, heads_enc, EH)
    value_heads = value_sum.astype(jnp.bfloat16).reshape(spans, span_len, heads_enc, EH)
    scores = jnp.einsum(
        "cqhe,ckhe->chqk", query_heads, key_heads, preferred_element_type=jnp.float32
    ) / math.sqrt(EH)
    enc_weights = jax.nn.softmax(scores, axis=-1).astype(jnp.bfloat16)
    head_mix = jnp.einsum(
        "chqk,ckhe->cqhe", enc_weights, value_heads, preferred_element_type=jnp.float32
    )
    head_mix = head_mix.astype(jnp.bfloat16).reshape(key_rows, width)
    full_mix = lax.all_gather(head_mix, TENSOR, axis=1, tiled=True)
    sliced = full_mix
    output_sum = jnp.dot(
        sliced, gathered_copies(wo_enc, "enc", 0), preferred_element_type=jnp.float32
    )
    encoded = (
        (flat_neighbour.astype(jnp.float32) + output_sum)
        .astype(jnp.bfloat16)
        .reshape(spans, keys_each, width)
    )
    carried = from_behind(encoded[spans - 1], "enc", 1)
    previous_part = jnp.concatenate([carried[None], encoded[: spans - 1]], axis=0).reshape(
        key_rows, width
    )
    previous = lax.all_gather(previous_part, TENSOR, axis=1, tiled=True)
    key_weight, value_weight = in_one_piece((wk_dec, wv_dec), ("dp", "enc"), 0, 1)
    dec_key = jnp.dot(previous, key_weight, preferred_element_type=jnp.float32).astype(jnp.bfloat16)
    dec_value = jnp.dot(previous, value_weight, preferred_element_type=jnp.float32).astype(
        jnp.bfloat16
    )
    heads_dec = queries.shape[1] // HD
    query_dec = queries.reshape(spans, span_len, heads_dec, HD)
    key_dec = dec_key.reshape(spans, keys_each, heads_dec, HD)
    value_dec = dec_value.reshape(spans, keys_each, heads_dec, HD)
    dec_scores = jnp.einsum(
        "cmhd,ckhd->chmk", query_dec, key_dec, preferred_element_type=jnp.float32
    ) / math.sqrt(HD)
    probs = jax.nn.softmax(dec_scores, axis=-1)
    probs_low = probs.astype(jnp.bfloat16)
    position = lax.axis_index("enc") * row_count + jnp.arange(row_count, dtype=jnp.int32)
    live_mask = jnp.logical_and(position < lengths[0], position >= span_len).reshape(
        spans, span_len, 1, 1
    )
    attended = jnp.einsum(
        "chmk,ckhd->cmhd", probs_low, value_dec, preferred_element_type=jnp.float32
    )
    attended = jnp.where(live_mask, attended, 0.0).astype(jnp.bfloat16).reshape(row_count, -1)
    cotangent = jnp.where(
        live_mask, grad_out.reshape(spans, span_len, heads_dec, HD), jnp.zeros((), jnp.bfloat16)
    )
    grad_value = jnp.einsum(
        "chmk,cmhd->ckhd", probs_low, cotangent, preferred_element_type=jnp.float32
    ).astype(jnp.bfloat16)
    grad_probs = jnp.einsum(
        "cmhd,ckhd->chmk", cotangent, value_dec, preferred_element_type=jnp.float32
    )
    inner = jnp.sum(grad_probs * probs, axis=-1, keepdims=True)
    grad_scores = (probs * (grad_probs - inner) / math.sqrt(HD)).astype(jnp.bfloat16)
    grad_key = jnp.einsum(
        "chmk,cmhd->ckhd", grad_scores, query_dec, preferred_element_type=jnp.float32
    ).astype(jnp.bfloat16)
    partial_value = jnp.einsum(
        "nd,ed->ne", grad_key.reshape(key_rows, -1), key_weight, preferred_element_type=jnp.float32
    )
    partial_value = partial_value + jnp.einsum(
        "nd,ed->ne",
        grad_value.reshape(key_rows, -1),
        value_weight,
        preferred_element_type=jnp.float32,
    )
    returned = (
        summed_rows(partial_value.astype(jnp.bfloat16), TENSOR, (1, 0), 1)
        .astype(jnp.float32)
        .reshape(spans, keys_each, width)
    )
    following = from_behind(returned[0].astype(jnp.bfloat16), "enc", -1).astype(jnp.float32)
    grad_encoded = jnp.concatenate([returned[1:], following[None]], axis=0)
    return (attended, grad_encoded)


def solution(mesh):
    split = Mesh(
        mesh.devices.reshape(mesh.shape["dp"], 2, 4, mesh.shape["enc"]),
        ("dp", "tensor_0", "tensor_1", "enc"),
    )
    in_specs = (
        P(("dp", "enc"), TENSOR),
        P(("dp", "enc"), None, TENSOR),
        P("dp"),
        P("enc", TENSOR),
        P("enc", TENSOR),
        P("enc", TENSOR),
        P("enc", TENSOR),
        P(("dp", "enc"), TENSOR),
        P(("dp", "enc"), TENSOR),
        P(("dp", "enc"), TENSOR),
        P(("dp", "enc"), TENSOR),
    )
    out_specs = (P(("dp", "enc"), TENSOR), P(("dp", "enc"), None, TENSOR))
    return jax.shard_map(
        on_device, mesh=split, in_specs=in_specs, out_specs=out_specs, check_vma=False
    )
```

profile of v0, /device:TPU:1, one launch (start us, length us, event | category | flops | bytes accessed | tf_op | source)
XLA Modules:
  0.0 678.9 jit_solution(7648377399311561809)
XLA Ops:
  7.2 1.0 copy.55
  8.2 1.7 pad_maximum_fusion
  10.0 1.7 pad_maximum_fusion.1
  11.7 0.8 broadcast_in_dim.43
  12.5 14.0 %all-to-all-start = ((bf16[16,64,128]{2,1,0:T(8,128)(2,1)}), bf16[16,64,128]{2,1,0:T(8,128)(2,1)S(1)}, u32[]{:S(2)}, u32[]{:S(2)}) async-start(bf16[16,64,128]{2,1,0:T(8,128)(2,1)} %broadcast_in_dim.43), calls=%async_computation | async-start | bytes 524288 | tf_op jit(solution)/shard_map/all_to_all | solution.py:31
  26.5 135.1 %all-gather.15.cloned.1.call-done = bf16[1572864]{0:T(1024)(128)(2,1)} async-done(((bf16[196608]{0:T(1024)(128)(2,1)}), bf16[1572864]{0:T(1024)(128)(2,1)}) %all-gather.15.cloned.1.call-update) | async-done | bytes 3145744 | tf_op jit(solution)/shard_map/all_gather | solution.py:21
  161.7 3.2 reshape.126
  164.9 1.2 slice.54
  166.1 0.8 copy-done
  166.9 1.8 convolution_convert_fusion.3
  168.9 2.7 copy.56
  171.6 93.4 %all-gather.7.cloned.1.call-done = bf16[8192,256]{1,0:T(8,128)(2,1)} async-done(((bf16[512,256]{1,0:T(8,128)(2,1)}), bf16[8192,256]{1,0:T(8,128)(2,1)}) %all-gather.7.cloned.1.call-update) | async-done | bytes 4194320 | tf_op jit(solution)/shard_map/all_gather | solution.py:41
  265.0 3.1 fusion.50
  268.5 2.3 fusion.47
  270.9 0.2 fusion.46
  271.3 0.7 copy.58
  272.1 0.6 pad_maximum_fusion.3
  272.8 27.9 %all_to_all.10 = bf16[16,64,128]{2,1,0:T(8,128)(2,1)S(1)} all-to-all(bf16[16,64,128]{2,1,0:T(8,128)(2,1)S(1)} %broadcast_in_dim.44), channel_id=1, replica_groups=mesh['dp'=4,'tensor_0'=2,'tensor_1'=4,'enc'=16] {'enc'}, dimensions={0} | all-to-all | bytes 524288 | tf_op jit(solution)/shard_map/all_to_all | solution.py:31
  300.8 63.7 %all-gather.9.cloned.1.call-done = bf16[512,1024]{0,1:T(8,128)(2,1)} async-done(((bf16[512,128]{0,1:T(8,128)(2,1)}), bf16[512,1024]{0,1:T(8,128)(2,1)}) %all-gather.9.cloned.1.call-update) | async-done | bytes 1048592 | tf_op jit(solution)/shard_map/all_gather | solution.py:112
  364.5 1.7 fusion.45
  366.2 1.9 collective-permute-start
  368.1 2.3 collective-permute-done
  370.4 0.7 pad_maximum_fusion.2
  372.2 109.5 %all-gather.13.cloned.1.call-done = bf16[1024,2048]{1,0:T(8,128)(2,1)} async-done(((bf16[16,2048]{1,0:T(8,128)(2,1)}), bf16[1024,2048]{1,0:T(8,128)(2,1)}) %all-gather.13.cloned.1.call-update) | async-done | bytes 4194320 | tf_op jit(solution)/shard_map/all_gather | solution.py:41
  481.6 85.6 %all-gather.11.cloned.1.call-done = bf16[512,1024]{1,0:T(8,128)(2,1)} async-done(((bf16[512,128]{1,0:T(8,128)(2,1)}), bf16[512,1024]{1,0:T(8,128)(2,1)}) %all-gather.11.cloned.1.call-update) | async-done | bytes 1048592 | tf_op jit(solution)/shard_map/all_gather | solution.py:126
  567.2 3.3 fusion.27
  570.5 0.3 copy.61
  570.8 0.9 copy-done.13
  571.7 1.3 fusion.30
  573.0 0.3 copy.59
  573.3 0.5 fusion.39
  573.8 1.2 fusion.84
  575.0 3.2 fusion.25
  578.1 2.4 copy.51
  580.6 1.5 fusion.62
  582.1 8.7 %fusion.24 = bf16[2,256,8,128]{3,1,2,0:T(8,128)(2,1)} fusion(f32[2,8,64,256]{3,2,1,0:T(8,128)S(1)} %fusion.62, bf16[2,64,8,128]{3,2,1,0:T(8,128)(2,1)S(1)} %bitcast.103, f32[2,8,64,256]{3,2,1,0:T(8,128)} %get-tuple-element.7, f32[2,8,64]{2,1,0:T(8,128)S(1)} %get-tuple-element.6), kind=kOutput, calls=%fused_computation.21 | convolution fusion | flops 69469440 | bytes 3411968 | tf_op jit(solution)/shard_map/chmk,cmhd->ckhd/dot_general | solution.py:160
  590.8 2.0 copy.50
  592.8 3.0 fusion.7
  595.8 1.3 fusion.33
  597.1 0.3 copy.66
  597.4 1.2 copy.52
  598.7 22.4 %reduce-scatter.3.cloned.1.call-done = bf16[2,512,128]{2,1,0:T(8,128)(2,1)} async-done(((bf16[8,512,128]{2,1,0:T(8,128)(2,1)}), bf16[2,512,128]{2,1,0:T(8,128)(2,1)}) %reduce-scatter.3.cloned.1.call-update) | async-done | bytes 262160 | tf_op jit(solution)/shard_map/reduce_scatter | solution.py:59
  621.1 43.8 %reduce-scatter.5.cloned.1.call-done = bf16[1,512,128]{2,1,0:T(8,128)(2,1)} async-done(((bf16[2,512,128]{2,1,0:T(8,128)(2,1)}), bf16[1,512,128]{2,1,0:T(8,128)(2,1)}) %reduce-scatter.5.cloned.1.call-update) | async-done | bytes 131088 | tf_op jit(solution)/shard_map/reduce_scatter | solution.py:59
  664.9 0.9 fusion.81
  665.8 2.6 collective-permute-start.1
  668.4 1.9 fusion.43
  670.4 0.8 copy.99
  671.3 0.7 maximum_convert_fusion
  (56 shorter events, 1.9 us)
Async XLA Ops:
  7.2 4.5 copy-start.9
  7.2 154.5 %all-gather.15.cloned.1.call-start = ((), (), s32[]{:S(2)}) async-start(), calls=%async_computation.10 | async-start | bytes 3538944 | tf_op jit(solution)/shard_map/all_gather | solution.py:21
  9.9 255.1 %all-gather.7.cloned.1.call-start = ((), (), s32[]{:S(2)}) async-start(), calls=%async_computation.4 | async-start | bytes 4456448 | tf_op jit(solution)/shard_map/all_gather | solution.py:41
  12.5 154.4 %all-to-all-start = ((bf16[16,64,128]{2,1,0:T(8,128)(2,1)}), bf16[16,64,128]{2,1,0:T(8,128)(2,1)S(1)}, u32[]{:S(2)}, u32[]{:S(2)}) async-start(bf16[16,64,128]{2,1,0:T(8,128)(2,1)} %broadcast_in_dim.43), calls=%async_computation | async-start | bytes 524288 | tf_op jit(solution)/shard_map/all_to_all | solution.py:31
  26.5 338.0 %all-gather.9.cloned.1.call-start = ((), (), s32[]{:S(2)}) async-start(), calls=%async_computation.5 | async-start | bytes 1179648 | tf_op jit(solution)/shard_map/all_gather | solution.py:112
  164.9 2.0 copy-start
  166.9 2.0 slice-start
  265.0 3.5 copy-start.1
  268.5 3.6 copy-start.7
  268.5 3.6 copy-start.8
  270.8 2.0 copy-start.10
  270.8 93.7 %copy-start.4 = (bf16[2,256,128]{2,1,0:T(8,128)(2,1)S(1)}, bf16[2,256,128]{2,1,0:T(8,128)(2,1)}, u32[]{:S(2)}) copy-start(bf16[2,256,128]{2,1,0:T(8,128)(2,1)} %param.12) | copy-start | bytes 393220
  271.1 100.9 %copy-start.5 = (bf16[128,1024]{1,0:T(8,128)(2,1)S(1)}, bf16[128,1024]{1,0:T(8,128)(2,1)}, u32[]{:S(2)}) copy-start(bf16[128,1024]{1,0:T(8,128)(2,1)} %param.20) | copy-start | bytes 786436
  271.3 100.8 %copy-start.6 = (bf16[128,1024]{1,0:T(8,128)(2,1)S(1)}, bf16[128,1024]{1,0:T(8,128)(2,1)}, u32[]{:S(2)}) copy-start(bf16[128,1024]{1,0:T(8,128)(2,1)} %param.21) | copy-start | bytes 786436
  272.0 209.6 %all-gather.13.cloned.1.call-start = ((), (), s32[]{:S(2)}) async-start(), calls=%async_computation.7 | async-start | bytes 4259840 | tf_op jit(solution)/shard_map/all_gather | solution.py:41
  272.7 294.5 %all-gather.11.cloned.1.call-start = ((), (), s32[]{:S(2)}) async-start(), calls=%async_computation.6 | async-start | bytes 1179648 | tf_op jit(solution)/shard_map/all_gather | solution.py:126
  366.2 4.2 collective-permute-start
  371.1 249.9 %reduce-scatter.3.cloned.1.call-start = ((), (), s32[]{:S(2)}) async-start(), calls=%async_computation.8 | async-start | bytes 1310720 | tf_op jit(solution)/shard_map/reduce_scatter | solution.py:59
  372.1 202.9 %copy-start.2 = (bf16[16,8,8,128]{3,2,1,0:T(8,128)(2,1)}, bf16[16,8,8,128]{3,2,1,0:T(8,128)(2,1)S(1)}, u32[]{:S(2)}) copy-start(bf16[16,8,8,128]{3,2,1,0:T(8,128)(2,1)S(1)} %copy.63) | copy-start | bytes 786436
  567.2 3.6 copy-start.11
  570.5 1.2 copy-start.13
  590.8 2.0 copy-start.3
  592.8 3.0 copy-start.12
  598.6 66.3 %reduce-scatter.5.cloned.1.call-start = ((), (), s32[]{:S(2)}) async-start(), calls=%async_computation.9 | async-start | bytes 393216 | tf_op jit(solution)/shard_map/reduce_scatter | solution.py:59
  665.8 5.6 collective-permute-start.1
Sparse Core Ops, SparseCore 0:
  11.2 150.4 all-gather.14
  164.3 100.6 all-gather.6
  272.1 92.2 all-gather.8
  366.5 115.0 all-gather.12
  485.1 82.0 all-gather.10
  598.7 22.2 reduce-scatter.2
  623.8 40.9 reduce-scatter.4
where the time goes:
time: 680 us; the launch traced here: 679 us
  waiting for transfers between devices  556 us (82%)
  matrix products  33.9 us (5%)
  blocking collectives  27.9 us (4%)
  local copies, waits for them, and re-layouts  20.2 us (3%)
  starting transfers between devices  19 us (3%)
  between operations  15.2 us (2%)
    all_gather x2, waiting for transfers between devices, in_one_piece(): lax.all_gather(both, axis, axis=dim, tiled=True)  203 us
    all_gather x1, waiting for transfers between devices, one_gather(): lines, at, gathered = (lax.all_gather(vector, axis), 0, [])  135 us
    all_gather x1, waiting for transfers between devices, on_device(): previous = lax.all_gather(previous_part, TENSOR, axis=1, tiled=True)  85.6 us
    reduce_scatter x2, waiting for transfers between devices, sum_in_order(): blocks = lax.psum_scatter(blocks, axes[k], scatter_dimension=0, tiled=True)  66.2 us
    all_gather x1, waiting for transfers between devices, on_device(): full_mix = lax.all_gather(head_mix, TENSOR, axis=1, tiled=True)  63.7 us
    all_to_all x1, blocking collectives, copy_for_each(): return lax.all_to_all(copies, axis, split_axis=0, concat_axis=0, tiled=True)  27.9 us
    all_to_all x1, starting transfers between devices, copy_for_each(): return lax.all_to_all(copies, axis, split_axis=0, concat_axis=0, tiled=True)  14 us
  transfers between devices with their start and end apart: 10, of which 9 were waited for; matrix products, arithmetic and copies ran while one was open for 3% of the time, Pallas kernels for 0%

commit v1 on v0

--- a/solution.py
+++ b/solution.py
@@ -109,7 +109,9 @@
         "chqk,ckhe->cqhe", enc_weights, value_heads, preferred_element_type=jnp.float32
     )
     head_mix = head_mix.astype(jnp.bfloat16).reshape(key_rows, width)
-    full_mix = lax.all_gather(head_mix, TENSOR, axis=1, tiled=True)
+    full_mix = jnp.concatenate(
+        lax.all_to_all(jnp.stack([head_mix] * lax.axis_size(TENSOR)), TENSOR, 0, 0), axis=1
+    )
     sliced = full_mix
     output_sum = jnp.dot(
         sliced, gathered_copies(wo_enc, "enc", 0), preferred_element_type=jnp.float32

time: 680 us -> 612 us (0.900)
  waiting for transfers between devices: 556 us -> 460 us
  blocking collectives: 27.9 us -> 47.9 us
  starting transfers between devices: 19 us -> 28.8 us
    all_gather x1 -> x0, waiting for transfers between devices: 63.7 us -> none  [on_device(): full_mix = lax.all_gather(head_mix, TENSOR, axis=1, tiled=True)]
    all_gather x2, waiting for transfers between devices: 203 us -> 172 us  [in_one_piece(): lax.all_gather(both, axis, axis=dim, tiled=True)]
    all_to_all x1, blocking collectives: 27.9 us -> 47.9 us  [on_device(): lax.all_to_all(jnp.stack([head_mix] * lax.axis_size(TENSOR)), TENSOR, 0, 0)]
    all_to_all x1 -> x2, starting transfers between devices: 14 us -> 23.9 us  [copy_for_each(): return lax.all_to_all(copies, axis, split_axis=0, concat_axis=0, tiled=True)]
  transfers between devices with their start and end apart: 10 -> 10, of which waited for: 9 -> 8; matrix products, arithmetic and copies ran while one was open for 3% -> 4% of each run, Pallas kernels for 0% -> 0%
where the time goes in v1:
time: 612 us
  waiting for transfers between devices  460 us (75%)
  blocking collectives  47.9 us (8%)
  matrix products  32.6 us (5%)
  starting transfers between devices  28.8 us (5%)
  local copies, waits for them, and re-layouts  20.3 us (3%)
  between operations  15.2 us (2%)
  other arithmetic  6.67 us (1%)
    all_gather x2, waiting for transfers between devices, in_one_piece(): lax.all_gather(both, axis, axis=dim, tiled=True)  172 us
    all_gather x1, waiting for transfers between devices, one_gather(): lines, at, gathered = (lax.all_gather(vector, axis), 0, [])  135 us
    all_gather x1, waiting for transfers between devices, on_device(): previous = lax.all_gather(previous_part, TENSOR, axis=1, tiled=True)  85.2 us
    reduce_scatter x2, waiting for transfers between devices, sum_in_order(): blocks = lax.psum_scatter(blocks, axes[k], scatter_dimension=0, tiled=True)  66 us
    all_to_all x1, blocking collectives, on_device(): lax.all_to_all(jnp.stack([head_mix] * lax.axis_size(TENSOR)), TENSOR, 0, 0)  47.9 us
    all_to_all x2, starting transfers between devices, copy_for_each(): return lax.all_to_all(copies, axis, split_axis=0, concat_axis=0, tiled=True)  23.9 us
  transfers between devices with their start and end apart: 10, of which 8 were waited for; matrix products, arithmetic and copies ran while one was open for 4% of the time, Pallas kernels for 0%

profile of v1, /device:TPU:1, one launch (start us, length us, event | category | flops | bytes accessed | tf_op | source)
XLA Modules:
  0.0 611.7 jit_solution(5138663553229847480)
XLA Ops:
  7.2 1.0 copy.55
  8.2 1.7 pad_maximum_fusion
  10.0 1.7 pad_maximum_fusion.1
  11.8 0.6 pad_maximum_fusion.3
  12.5 0.8 broadcast_in_dim.43
  13.2 14.0 %all-to-all-start = ((bf16[16,64,128]{2,1,0:T(8,128)(2,1)}), bf16[16,64,128]{2,1,0:T(8,128)(2,1)S(1)}, u32[]{:S(2)}, u32[]{:S(2)}) async-start(bf16[16,64,128]{2,1,0:T(8,128)(2,1)} %broadcast_in_dim.43), calls=%async_computation | async-start | bytes 524288 | tf_op jit(solution)/shard_map/all_to_all | solution.py:31
  27.2 135.2 %all-gather.12.cloned.1.call-done = bf16[1572864]{0:T(1024)(128)(2,1)} async-done(((bf16[196608]{0:T(1024)(128)(2,1)}), bf16[1572864]{0:T(1024)(128)(2,1)}) %all-gather.12.cloned.1.call-update) | async-done | bytes 3145744 | tf_op jit(solution)/shard_map/all_gather | solution.py:21
  162.5 3.2 reshape.132
  165.7 1.1 slice.54
  166.8 0.8 copy-done
  167.7 0.8 broadcast_in_dim.44
  168.4 9.8 %all-to-all-start.2 = ((bf16[16,64,128]{2,1,0:T(8,128)(2,1)}), bf16[16,64,128]{2,1,0:T(8,128)(2,1)S(1)}, u32[]{:S(2)}, u32[]{:S(2)}) async-start(bf16[16,64,128]{2,1,0:T(8,128)(2,1)} %broadcast_in_dim.44), calls=%async_computation.2 | async-start | bytes 524288 | tf_op jit(solution)/shard_map/all_to_all | solution.py:31
  178.3 1.7 convolution_convert_fusion.3
  180.2 2.8 copy.56
  182.9 85.2 %all-gather.6.cloned.1.call-done = bf16[8192,256]{1,0:T(8,128)(2,1)} async-done(((bf16[512,256]{1,0:T(8,128)(2,1)}), bf16[8192,256]{1,0:T(8,128)(2,1)}) %all-gather.6.cloned.1.call-update) | async-done | bytes 4194320 | tf_op jit(solution)/shard_map/all_gather | solution.py:41
  268.1 3.1 fusion.50
  271.3 2.3 fusion.47
  274.5 47.9 %all_to_all.15 = bf16[8,512,128]{1,2,0:T(8,128)(2,1)S(1)} all-to-all(bf16[8,512,128]{1,2,0:T(8,128)(2,1)S(1)} %stack.3), channel_id=1, replica_groups=mesh['dp'=4,'tensor_0'=2,'tensor_1'=4,'enc'=16] {'tensor_0','tensor_1'}, dimensions={0} | all-to-all | bytes 2097152 | tf_op jit(solution)/shard_map/all_to_all | solution.py:113
  322.4 0.5 fusion.45
  322.9 1.9 collective-permute-start
  324.8 1.3 collective-permute-done
  326.1 0.7 pad_maximum_fusion.2
  326.8 0.2 reduce-scatter.3.cloned.1.call-start
  327.8 87.1 %all-gather.10.cloned.1.call-done = bf16[1024,2048]{1,0:T(8,128)(2,1)} async-done(((bf16[16,2048]{1,0:T(8,128)(2,1)}), bf16[1024,2048]{1,0:T(8,128)(2,1)}) %all-gather.10.cloned.1.call-update) | async-done | bytes 4194320 | tf_op jit(solution)/shard_map/all_gather | solution.py:41
  415.0 85.2 %all-gather.8.cloned.1.call-done = bf16[512,1024]{1,0:T(8,128)(2,1)} async-done(((bf16[512,128]{1,0:T(8,128)(2,1)}), bf16[512,1024]{1,0:T(8,128)(2,1)}) %all-gather.8.cloned.1.call-update) | async-done | bytes 1048592 | tf_op jit(solution)/shard_map/all_gather | solution.py:128
  500.2 3.3 fusion.27
  503.5 0.3 copy.61
  503.8 0.9 copy-done.13
  504.7 1.3 fusion.30
  506.0 0.3 copy.59
  506.2 0.5 fusion.39
  506.7 1.2 fusion.84
  507.9 3.2 fusion.25
  511.1 2.4 copy.51
  513.5 1.5 fusion.62
  515.0 8.7 %fusion.24 = bf16[2,256,8,128]{3,1,2,0:T(8,128)(2,1)} fusion(f32[2,8,64,256]{3,2,1,0:T(8,128)S(1)} %fusion.62, bf16[2,64,8,128]{3,2,1,0:T(8,128)(2,1)S(1)} %bitcast.107, f32[2,8,64,256]{3,2,1,0:T(8,128)} %get-tuple-element.7, f32[2,8,64]{2,1,0:T(8,128)S(1)} %get-tuple-element.6), kind=kOutput, calls=%fused_computation.21 | convolution fusion | flops 69469440 | bytes 3411968 | tf_op jit(solution)/shard_map/chmk,cmhd->ckhd/dot_general | solution.py:162
  523.7 2.0 copy.50
  525.7 3.0 fusion.7
  528.8 1.3 fusion.33
  530.1 0.3 copy.66
  530.3 1.1 copy.52
  531.6 22.4 %reduce-scatter.3.cloned.1.call-done = bf16[2,512,128]{2,1,0:T(8,128)(2,1)} async-done(((bf16[8,512,128]{2,1,0:T(8,128)(2,1)}), bf16[2,512,128]{2,1,0:T(8,128)(2,1)}) %reduce-scatter.3.cloned.1.call-update) | async-done | bytes 262160 | tf_op jit(solution)/shard_map/reduce_scatter | solution.py:59
  554.0 43.6 %reduce-scatter.5.cloned.1.call-done = bf16[1,512,128]{2,1,0:T(8,128)(2,1)} async-done(((bf16[2,512,128]{2,1,0:T(8,128)(2,1)}), bf16[1,512,128]{2,1,0:T(8,128)(2,1)}) %reduce-scatter.5.cloned.1.call-update) | async-done | bytes 131088 | tf_op jit(solution)/shard_map/reduce_scatter | solution.py:59
  597.6 0.9 fusion.81
  598.5 2.6 collective-permute-start.1
  601.1 1.9 fusion.43
  603.2 0.8 copy.99
  604.1 0.7 maximum_convert_fusion
  (56 shorter events, 1.9 us)
Async XLA Ops:
  7.2 4.6 copy-start.7
  7.2 4.6 copy-start.8
  7.2 5.3 copy-start.9
  7.2 155.3 %all-gather.12.cloned.1.call-start = ((), (), s32[]{:S(2)}) async-start(), calls=%async_computation.10 | async-start | bytes 3538944 | tf_op jit(solution)/shard_map/all_gather | solution.py:21
  9.9 258.2 %all-gather.6.cloned.1.call-start = ((), (), s32[]{:S(2)}) async-start(), calls=%async_computation.5 | async-start | bytes 4456448 | tf_op jit(solution)/shard_map/all_gather | solution.py:41
  11.7 403.2 %all-gather.10.cloned.1.call-start = ((), (), s32[]{:S(2)}) async-start(), calls=%async_computation.7 | async-start | bytes 4259840 | tf_op jit(solution)/shard_map/all_gather | solution.py:41
  13.2 154.5 %all-to-all-start = ((bf16[16,64,128]{2,1,0:T(8,128)(2,1)}), bf16[16,64,128]{2,1,0:T(8,128)(2,1)S(1)}, u32[]{:S(2)}, u32[]{:S(2)}) async-start(bf16[16,64,128]{2,1,0:T(8,128)(2,1)} %broadcast_in_dim.43), calls=%async_computation | async-start | bytes 524288 | tf_op jit(solution)/shard_map/all_to_all | solution.py:31
  165.7 2.0 copy-start
  166.8 0.8 copy-start.10
  167.7 12.5 %slice-start = ((bf16[8,196608]{1,0:T(8,128)(2,1)}), bf16[8,131072]{1,0:T(8,128)(2,1)S(1)}, s32[]{:S(2)}) async-start(bf16[8,196608]{1,0:T(8,128)(2,1)} %copy-done), calls=%async_computation.11 | async-start | bytes 4194304 | tf_op jit(solution)/shard_map/slice | solution.py:23
  168.4 105.9 %all-to-all-start.2 = ((bf16[16,64,128]{2,1,0:T(8,128)(2,1)}), bf16[16,64,128]{2,1,0:T(8,128)(2,1)S(1)}, u32[]{:S(2)}, u32[]{:S(2)}) async-start(bf16[16,64,128]{2,1,0:T(8,128)(2,1)} %broadcast_in_dim.44), calls=%async_computation.2 | async-start | bytes 524288 | tf_op jit(solution)/shard_map/all_to_all | solution.py:31
  178.3 321.9 %all-gather.8.cloned.1.call-start = ((), (), s32[]{:S(2)}) async-start(), calls=%async_computation.6 | async-start | bytes 1179648 | tf_op jit(solution)/shard_map/all_gather | solution.py:128
  268.1 3.2 copy-start.1
  274.2 48.2 %copy-start.4 = (bf16[2,256,128]{2,1,0:T(8,128)(2,1)S(1)}, bf16[2,256,128]{2,1,0:T(8,128)(2,1)}, u32[]{:S(2)}) copy-start(bf16[2,256,128]{2,1,0:T(8,128)(2,1)} %param.12) | copy-start | bytes 393220
  274.5 53.2 %copy-start.5 = (bf16[128,1024]{1,0:T(8,128)(2,1)S(1)}, bf16[128,1024]{1,0:T(8,128)(2,1)}, u32[]{:S(2)}) copy-start(bf16[128,1024]{1,0:T(8,128)(2,1)} %param.20) | copy-start | bytes 786436
  274.5 53.3 %copy-start.6 = (bf16[128,1024]{1,0:T(8,128)(2,1)S(1)}, bf16[128,1024]{1,0:T(8,128)(2,1)}, u32[]{:S(2)}) copy-start(bf16[128,1024]{1,0:T(8,128)(2,1)} %param.21) | copy-start | bytes 786436
  322.9 3.2 collective-permute-start
  326.8 227.2 %reduce-scatter.3.cloned.1.call-start = ((), (), s32[]{:S(2)}) async-start(), calls=%async_computation.8 | async-start | bytes 1310720 | tf_op jit(solution)/shard_map/reduce_scatter | solution.py:59
  327.8 180.1 %copy-start.2 = (bf16[16,8,8,128]{3,2,1,0:T(8,128)(2,1)}, bf16[16,8,8,128]{3,2,1,0:T(8,128)(2,1)S(1)}, u32[]{:S(2)}) copy-start(bf16[16,8,8,128]{3,2,1,0:T(8,128)(2,1)S(1)} %copy.63) | copy-start | bytes 786436
  500.2 3.6 copy-start.11
  503.5 1.2 copy-start.13
  523.7 2.0 copy-start.3
  525.7 3.1 copy-start.12
  531.5 66.1 %reduce-scatter.5.cloned.1.call-start = ((), (), s32[]{:S(2)}) async-start(), calls=%async_computation.9 | async-start | bytes 393216 | tf_op jit(solution)/shard_map/reduce_scatter | solution.py:59
  598.5 5.6 collective-permute-start.1
Sparse Core Ops, SparseCore 0:
  11.2 151.2 all-gather.11
  165.1 102.9 all-gather.5
  270.3 144.6 all-gather.9
  418.4 81.6 all-gather.7
  531.6 22.2 reduce-scatter.2
  556.6 40.9 reduce-scatter.4
